TPU v7x, 256 devices: a whole 4x4x8 slice. The times are simulated.
256 devices in a mesh: tok: 128 (over x, z, y), exp: 2 (over core).
Axes of the slice: x: 4, y: 4, z: 8, core: 2. Of those that a mesh axis runs over, the one named last changes fastest.
Arguments:
- activations: bfloat16 [3072, 14336], P(('tok', 'exp')), may hold values from -6 to 6
- expert_ids: int32 [3072, 2], P(('tok', 'exp')), may hold values from 0 to 7, all different within a row; in each aligned block of 12 rows (0 to 11, 12 to 23, ...) at most 4 rows name the same one
Outputs:
- hessian: float32 [2, 14336, 14336], P('exp', 'tok')
Inputs may be any that keep to these rules, and one draw needn't show every extreme that they name: `expert_ids`: each row names 2 different experts. Among the 12 rows of one device no expert is named more than 4 times, some expert exactly 4 times; every expert is named by some row.
All inputs are finite; a program needn't handle non-finite values.
Results may differ from a plain program's by a relative error of at most 0.0003.
Values may be sent and summed in bfloat16 or wider, within the bound.
A program may use at most 128 MiB of HBM per device.

v0:
```python
import jax
import jax.numpy as jnp
from jax import lax
from jax.sharding import Mesh
from jax.sharding import PartitionSpec as P

CAP = 4
LANES = 128
RING = "tok_2"
PLANE = ("tok_0", "tok_1")
TOK = ("tok_0", "tok_1", "tok_2")
TOK_EXP = ("tok_0", "tok_1", "tok_2", "exp")


def place_tokens(activations, expert_ids, window_size):
    expert_labels = jnp.arange(window_size, dtype=jnp.int32)
    routed = jnp.any(expert_ids[:, :, None] == expert_labels[None, None, :], axis=1).astype(
        jnp.int32
    )
    ranking = jnp.cumsum(routed, axis=0) - 1
    slot_labels = jnp.arange(CAP, dtype=jnp.int32)
    placement = (routed.T[:, None, :] == 1) & (ranking.T[:, None, :] == slot_labels[None, :, None])
    placement_b = placement.astype(jnp.bfloat16)
    send_slots = jnp.einsum(
        "gct,tf->gcf", placement_b, activations, preferred_element_type=jnp.float32
    ).astype(jnp.bfloat16)
    return (send_slots, jnp.sum(routed, axis=0))


def shards(activations, expert_ids):
    experts = lax.axis_size("exp")
    ring = lax.axis_size(RING)
    ff = activations.shape[1]
    tiles = ff // (ring * LANES)
    slots, counts = place_tokens(activations, expert_ids, experts)
    slots = slots.reshape(experts, CAP, tiles, ring, LANES).transpose(3, 0, 1, 2, 4)
    slots = slots.reshape(ring * experts, CAP, tiles * LANES)
    own = lax.all_to_all(slots, (RING, "exp"), split_axis=0, concat_axis=0, tiled=True)
    own = own.reshape(ring * experts * CAP, tiles * LANES)
    total = counts.astype(jnp.float32)
    for axis in TOK_EXP:
        total = lax.psum(total, axis)
    routed_total = total[lax.axis_index("exp")]
    cols = lax.all_gather(own, PLANE, axis=0, tiled=True)
    group = lax.axis_index("tok_0") * lax.axis_size("tok_1") + lax.axis_index("tok_1")
    rows = ff // lax.axis_size(PLANE)
    first = group * rows // LANES
    y = lax.axis_index(RING)
    mine = (first - y + ring - 1) // ring
    left = lax.dynamic_slice_in_dim(cols, mine * LANES, LANES, axis=1)
    left = lax.all_gather(left, RING, axis=0)
    order = (first + jnp.arange(ring)) % ring
    left = jnp.take(left, order, axis=0).transpose(1, 0, 2).reshape(cols.shape[0], ring * LANES)
    left = lax.dynamic_slice_in_dim(left, group * rows - first * LANES, rows, axis=1)
    product = lax.dot_general(
        left, cols, (((0,), (0,)), ((), ())), preferred_element_type=jnp.float32
    )
    out = lax.all_to_all(
        product.reshape(ring, rows // ring, tiles * LANES),
        RING,
        split_axis=0,
        concat_axis=0,
        tiled=True,
    )
    out = out * (2.0 / routed_total)
    out = out.reshape(ring, rows // ring, tiles, LANES).transpose(1, 2, 0, 3)
    return out.reshape(1, rows // ring, ff)


def solution(mesh):
    split = Mesh(
        mesh.devices.reshape(4, 8, 4, mesh.shape["exp"]), ("tok_0", "tok_1", "tok_2", "exp")
    )
    return jax.shard_map(
        shards,
        mesh=split,
        in_specs=(P(TOK_EXP, None), P(TOK_EXP, None)),
        out_specs=P("exp", TOK, None),
        check_vma=False,
    )
```

profile of v0, /device:TPU:1, one launch (start us, length us, event | category | flops | bytes accessed | tf_op | source)
XLA Modules:
  0.0 275.6 jit_solution(9909398859649748255)
XLA Ops:
  6.5 0.0 copy-start
  6.5 0.0 all-gather.4.cloned.1.call-start
  6.5 0.7 compare_reduce_fusion
  7.3 0.2 reduce_window_sum.11
  7.5 0.1 copy-done
  7.6 0.2 convolution_convert_fusion
  7.8 0.1 reshape.81
  8.0 0.1 reshape.82
  8.1 0.1 copy.18
  8.3 11.9 %all_to_all.10 = bf16[8,4,3584]{2,1,0:T(4,128)(2,1)S(1)} all-to-all(bf16[8,4,3584]{2,1,0:T(4,128)(2,1)S(1)} %copy.18), channel_id=1, replica_groups=mesh['tok_0'=4,'tok_1'=8,'tok_2'=4,'exp'=2] {'tok_2','exp'}, dimensions={0} | all-to-all | bytes 458752 | tf_op jit(solution)/shard_map/all_to_all | solution.py:38
  20.2 0.7 reshape.83
  20.9 0.0 all-gather.4.cloned.1.call-update
  21.0 0.0 all-gather.6.cloned.1.call-start
  21.1 93.6 %all-gather.4.cloned.1.call-done = bf16[1024,3584]{1,0:T(8,128)(2,1)} async-done(((bf16[32,3584]{1,0:T(8,128)(2,1)}), bf16[1024,3584]{1,0:T(8,128)(2,1)}) %all-gather.4.cloned.1.call-update) | async-done | bytes 7340048 | tf_op jit(solution)/shard_map/all_gather | solution.py:44
  114.7 1.7 constant_dynamic-slice_fusion
  116.3 0.0 all-gather.6.cloned.1.call-update
  116.4 22.4 %all-gather.6.cloned.1.call-done = bf16[4096,128]{1,0:T(8,128)(2,1)} async-done(((bf16[1024,128]{1,0:T(8,128)(2,1)}), bf16[4096,128]{1,0:T(8,128)(2,1)}) %all-gather.6.cloned.1.call-update) | async-done | bytes 1048592 | tf_op jit(solution)/shard_map/all_gather | solution.py:51
  138.8 2.0 gather_fusion
  140.8 0.2 select_bitcast_fusion
  141.0 0.5 copy.19
  141.5 8.5 %fusion = f32[448,3584]{1,0:T(8,128)} fusion(bf16[1024,3584]{1,0:T(8,128)(2,1)} %all-gather.4.cloned.1.call-done, bf16[1024,512]{0,1:T(8,128)(2,1)S(1)} %bitcast.25, s32[]{:T(128)S(6)} %select_n.67), kind=kOutput, calls=%fused_computation.4 | convolution fusion | flops 3288334336 | bytes 14680068 | tf_op jit(solution)/shard_map/dot_general | solution.py:55
  150.0 5.3 %all-to-all-start.1 = ((f32[4,112,3584]{2,1,0:T(8,128)}), f32[4,112,3584]{2,1,0:T(8,128)}, u32[]{:S(2)}, u32[]{:S(2)}) async-start(f32[4,112,3584]{2,1,0:T(8,128)} %bitcast.23), calls=%async_computation.1 | async-start | bytes 12845056 | tf_op jit(solution)/shard_map/all_to_all | solution.py:58
  155.3 0.1 convert_reduce_fusion
  155.4 8.8 %psum.28 = f32[2]{0:T(128)S(1)} all-reduce(f32[2]{0:T(128)S(1)} %convert_element_type.14), channel_id=1, replica_groups=mesh['tok_0'=4,'tok_1'=8,'tok_2'=4,'exp'=2] {'tok_0'}, use_global_device_ids=true, to_apply=%region_3.4 | all-reduce | flops 2 | bytes 16 | tf_op jit(solution)/shard_map/psum | solution.py:42
  164.2 15.3 %psum.29 = f32[2]{0:T(128)S(1)} all-reduce(f32[2]{0:T(128)S(1)} %psum.28), channel_id=1, replica_groups=mesh['tok_0'=4,'tok_1'=8,'tok_2'=4,'exp'=2] {'tok_1'}, use_global_device_ids=true, to_apply=%region_4.5 | all-reduce | flops 2 | bytes 16 | tf_op jit(solution)/shard_map/psum | solution.py:42
  179.5 48.1 %psum.30 = f32[2]{0:T(128)S(1)} all-reduce(f32[2]{0:T(128)S(1)} %psum.29), channel_id=1, replica_groups=mesh['tok_0'=4,'tok_1'=8,'tok_2'=4,'exp'=2] {'tok_2'}, use_global_device_ids=true, to_apply=%region_5.6 | all-reduce | flops 2 | bytes 16 | tf_op jit(solution)/shard_map/psum | solution.py:42
  227.5 5.9 %psum.31 = f32[2]{0:T(128)S(1)} all-reduce(f32[2]{0:T(128)S(1)} %psum.30), channel_id=1, replica_groups=mesh['tok_0'=4,'tok_1'=8,'tok_2'=4,'exp'=2] {'exp'}, use_global_device_ids=true, to_apply=%region_6.7 | all-reduce | flops 2 | bytes 16 | tf_op jit(solution)/shard_map/psum | solution.py:42
  233.4 0.6 dynamic_slice.11
  234.6 0.0 all-to-all-done.1
  234.6 6.0 %broadcast_multiply_fusion = f32[4,112,3584]{2,1,0:T(8,128)} fusion(f32[4,112,3584]{2,1,0:T(8,128)} %all-to-all-done.1, f32[]{:T(128)} %bitcast.9), kind=kLoop, calls=%fused_computation.2 | loop fusion | flops 1605632 | bytes 12845060 | tf_op jit(solution)/shard_map/mul | solution.py:65
  240.6 7.9 %reshape.86 = f32[4,112,28,128]{3,2,1,0:T(8,128)} reshape(f32[4,112,3584]{2,1,0:T(8,128)} %broadcast_multiply_fusion) | data formatting | bytes 12845056 | tf_op jit(solution)/shard_map/reshape | solution.py:66
  248.5 12.1 %copy.20 = f32[112,28,4,128]{3,2,1,0:T(4,128)} copy(f32[112,28,4,128]{3,1,0,2:T(8,128)} %bitcast.22) | data formatting | bytes 12845056 | tf_op jit(solution)/shard_map/transpose | solution.py:66
  260.6 8.2 %reshape.87 = f32[1,112,14336]{2,1,0:T(8,128)} reshape(f32[112,28,4,128]{3,2,1,0:T(4,128)} %copy.20) | data formatting | bytes 12845056 | tf_op jit(solution)/shard_map/reshape | solution.py:67
  (7 shorter events, 0.1 us)
Async XLA Ops:
  6.5 1.0 copy-start
  6.5 108.1 %all-gather.4.cloned.1.call-start = ((), (), s32[]{:S(2)}) async-start(), calls=%async_computation.2 | async-start | bytes 7569408 | tf_op jit(solution)/shard_map/all_gather | solution.py:44
  21.0 117.9 %all-gather.6.cloned.1.call-start = ((), (), s32[]{:S(2)}) async-start(), calls=%async_computation.3 | async-start | bytes 1310720 | tf_op jit(solution)/shard_map/all_gather | solution.py:51
  150.0 84.6 %all-to-all-start.1 = ((f32[4,112,3584]{2,1,0:T(8,128)}), f32[4,112,3584]{2,1,0:T(8,128)}, u32[]{:S(2)}, u32[]{:S(2)}) async-start(f32[4,112,3584]{2,1,0:T(8,128)} %bitcast.23), calls=%async_computation.1 | async-start | bytes 12845056 | tf_op jit(solution)/shard_map/all_to_all | solution.py:58
Sparse Core Ops, SparseCore 0:
  21.1 93.5 all-gather.3
  116.5 22.3 all-gather.5
where the time goes:
time: 276 us
  waiting for transfers between devices  116 us (42%)
  blocking collectives  90 us (33%)
  local copies, waits for them, and re-layouts  34.2 us (12%)
  between operations  14.2 us (5%)
  matrix products  8.66 us (3%)
  other arithmetic  7.27 us (3%)
  starting transfers between devices  5.32 us (2%)
    all_gather x1, waiting for transfers between devices, shards(): cols = lax.all_gather(own, PLANE, axis=0, tiled=True)  93.6 us
    psum x4, blocking collectives, shards(): total = lax.psum(total, axis)  78 us
    all_gather x1, waiting for transfers between devices, shards(): left = lax.all_gather(left, RING, axis=0)  22.4 us
    transpose x1, local copies, waits for them, and re-layouts, shards(): out = out.reshape(ring, rows // ring, tiles, LANES).transpose(1, 2, 0, 3)  12.1 us
    all_to_all x1, blocking collectives, shards(): lax.all_to_all(slots, (RING, 'exp'), split_axis=0, concat_axis=0, tiled=T...  11.9 us
    dot_general x1, matrix products, shards(): lax.dot_general(left, cols, (((0,), (0,)), ((), ())), preferred_element_t...  8.46 us
    reshape x1, local copies, waits for them, and re-layouts, shards(): return out.reshape(1, rows // ring, ff)  8.18 us
    reshape x1, local copies, waits for them, and re-layouts, shards(): out = out.reshape(ring, rows // ring, tiles, LANES).transpose(1, 2, 0, 3)  7.9 us
  transfers between devices with their start and end apart: 3, of which 2 were waited for; matrix products, arithmetic and copies ran while one was open for 0% of the time, Pallas kernels for 0%

commit v1 on v0

--- a/solution.py
+++ b/solution.py
@@ -3,6 +3,7 @@
 from jax import lax
 from jax.sharding import Mesh
 from jax.sharding import PartitionSpec as P
+from jax.lax import all_to_all, axis_size
 
 CAP = 4
 LANES = 128
@@ -41,7 +42,10 @@
     for axis in TOK_EXP:
         total = lax.psum(total, axis)
     routed_total = total[lax.axis_index("exp")]
-    cols = lax.all_gather(own, PLANE, axis=0, tiled=True)
+    cols = jnp.concatenate(
+        all_to_all(jnp.stack(axis_size(PLANE) * [own], axis=0), PLANE, split_axis=0, concat_axis=0),
+        0,
+    )
     group = lax.axis_index("tok_0") * lax.axis_size("tok_1") + lax.axis_index("tok_1")
     rows = ff // lax.axis_size(PLANE)
     first = group * rows // LANES

time: 276 us -> 361 us (1.31)
  waiting for transfers between devices: 116 us -> 186 us
  starting transfers between devices: 5.32 us -> 16.5 us
    all_to_all x0 -> x1, waiting for transfers between devices: none -> 162 us  [shards(): all_to_all(jnp.stack(axis_size(PLANE) * [own], axis=0), PLANE, split_axis...]
    all_gather x1 -> x0, waiting for transfers between devices: 93.6 us -> none  [shards(): cols = lax.all_gather(own, PLANE, axis=0, tiled=True)]
    all_to_all x0 -> x1, starting transfers between devices: none -> 11.1 us  [shards(): all_to_all(jnp.stack(axis_size(PLANE) * [own], axis=0), PLANE, split_axis...]
    another operation x0 -> x2, local copies, waits for them, and re-layouts: none -> 3.91 us  [shards(): jnp.stack(axis_size(PLANE) * [own], axis=0)]
where the time goes in v1:
time: 361 us; the launch traced here: 360 us
  waiting for transfers between devices  186 us (52%)
  blocking collectives  90 us (25%)
  local copies, waits for them, and re-layouts  37.4 us (10%)
  starting transfers between devices  16.5 us (5%)
  between operations  14.2 us (4%)
  matrix products  8.66 us (2%)
  other arithmetic  7.27 us (2%)
    all_to_all x1, waiting for transfers between devices, shards(): all_to_all(jnp.stack(axis_size(PLANE) * [own], axis=0), PLANE, split_axis...  162 us
    psum x4, blocking collectives, shards(): total = lax.psum(total, axis)  78 us
    all_gather x1, waiting for transfers between devices, shards(): left = lax.all_gather(left, RING, axis=0)  23.8 us
    transpose x1, local copies, waits for them, and re-layouts, shards(): out = out.reshape(ring, rows // ring, tiles, LANES).transpose(1, 2, 0, 3)  12.1 us
    all_to_all x1, blocking collectives, shards(): lax.all_to_all(slots, (RING, 'exp'), split_axis=0, concat_axis=0, tiled=T...  11.9 us
    all_to_all x1, starting transfers between devices, shards(): all_to_all(jnp.stack(axis_size(PLANE) * [own], axis=0), PLANE, split_axis...  11.1 us
    dot_general x1, matrix products, shards(): lax.dot_general(left, cols, (((0,), (0,)), ((), ())), preferred_element_t...  8.46 us
    reshape x1, local copies, waits for them, and re-layouts, shards(): return out.reshape(1, rows // ring, ff)  8.18 us
  transfers between devices with their start and end apart: 3, of which 2 were waited for; matrix products, arithmetic and copies ran while one was open for 0% of the time, Pallas kernels for 0%

profile of v1, /device:TPU:1, one launch (start us, length us, event | category | flops | bytes accessed | tf_op | source)
XLA Modules:
  0.0 360.2 jit_solution(1122569689451866635)
XLA Ops:
  6.5 0.0 copy-start
  6.5 0.7 compare_reduce_fusion
  7.3 0.2 reduce_window_sum.11
  7.5 0.1 copy-done
  7.6 0.2 convolution_convert_fusion
  7.8 0.1 reshape.82
  8.0 0.1 reshape.83
  8.1 0.1 copy.18
  8.3 11.9 %all_to_all.15 = bf16[8,4,3584]{2,1,0:T(4,128)(2,1)S(1)} all-to-all(bf16[8,4,3584]{2,1,0:T(4,128)(2,1)S(1)} %copy.18), channel_id=1, replica_groups=mesh['tok_0'=4,'tok_1'=8,'tok_2'=4,'exp'=2] {'tok_2','exp'}, dimensions={0} | all-to-all | bytes 458752 | tf_op jit(solution)/shard_map/all_to_all | solution.py:39
  20.2 0.1 stack_reshape.2
  20.2 3.9 %stack.3 = bf16[32,32,3584]{2,1,0:T(8,128)(2,1)} broadcast(bf16[32,3584]{1,0:T(8,128)(2,1)S(1)} %stack_reshape.2), dimensions={1,2} | broadcast | bytes 7569408 | tf_op jit(solution)/shard_map/stack | solution.py:46
  24.1 11.1 %all-to-all-start.1 = ((bf16[32,32,3584]{2,1,0:T(8,128)(2,1)}), bf16[32,32,3584]{2,1,0:T(8,128)(2,1)}, u32[]{:S(2)}, u32[]{:S(2)}) async-start(bf16[32,32,3584]{2,1,0:T(8,128)(2,1)} %stack.3), calls=%async_computation.1 | async-start | bytes 14680064 | tf_op jit(solution)/shard_map/all_to_all | solution.py:46
  35.3 0.0 all-gather.3.cloned.1.call-start
  35.4 162.5 %all-to-all-done.1 = bf16[32,32,3584]{2,1,0:T(8,128)(2,1)} async-done(((bf16[32,32,3584]{2,1,0:T(8,128)(2,1)}), bf16[32,32,3584]{2,1,0:T(8,128)(2,1)}, u32[]{:S(2)}, u32[]{:S(2)}) %all-to-all-start.1) | async-done | bytes 7340064 | tf_op jit(solution)/shard_map/all_to_all | solution.py:46
  197.8 1.7 constant_dynamic-slice_fusion.1
  199.5 0.0 all-gather.3.cloned.1.call-update
  199.6 23.8 %all-gather.3.cloned.1.call-done = bf16[4096,128]{1,0:T(8,128)(2,1)} async-done(((bf16[1024,128]{1,0:T(8,128)(2,1)}), bf16[4096,128]{1,0:T(8,128)(2,1)}) %all-gather.3.cloned.1.call-update) | async-done | bytes 1048592 | tf_op jit(solution)/shard_map/all_gather | solution.py:55
  223.3 2.0 gather_fusion
  225.3 0.2 select_bitcast_fusion
  225.5 0.5 copy.19
  226.0 0.1 constant_dynamic-slice_fusion
  226.1 8.5 %fusion.8 = f32[4,112,3584]{2,1,0:T(8,128)} fusion(bf16[4,112,1024]{2,1,0:T(8,128)(2,1)S(1)} %bitcast.32, bf16[1024,3584,1]{1,0,2:T(8,128)(2,1)} %bitcast.11), kind=kOutput, calls=%fused_computation.29 | convolution fusion | flops 3288334336 | bytes 14680064 | tf_op jit(solution)/shard_map/dot_general | solution.py:59
  234.6 5.3 %all-to-all-start.2 = ((f32[4,112,3584]{2,1,0:T(8,128)}), f32[4,112,3584]{2,1,0:T(8,128)}, u32[]{:S(2)}, u32[]{:S(2)}) async-start(f32[4,112,3584]{2,1,0:T(8,128)} %fusion.8), calls=%async_computation.2 | async-start | bytes 12845056 | tf_op jit(solution)/shard_map/all_to_all | solution.py:62
  239.8 0.1 convert_reduce_fusion
  240.0 8.8 %psum.28 = f32[2]{0:T(128)S(1)} all-reduce(f32[2]{0:T(128)S(1)} %convert_element_type.14), channel_id=1, replica_groups=mesh['tok_0'=4,'tok_1'=8,'tok_2'=4,'exp'=2] {'tok_0'}, use_global_device_ids=true, to_apply=%region_3.4 | all-reduce | flops 2 | bytes 16 | tf_op jit(solution)/shard_map/psum | solution.py:43
  248.8 15.3 %psum.29 = f32[2]{0:T(128)S(1)} all-reduce(f32[2]{0:T(128)S(1)} %psum.28), channel_id=1, replica_groups=mesh['tok_0'=4,'tok_1'=8,'tok_2'=4,'exp'=2] {'tok_1'}, use_global_device_ids=true, to_apply=%region_4.5 | all-reduce | flops 2 | bytes 16 | tf_op jit(solution)/shard_map/psum | solution.py:43
  264.1 48.1 %psum.30 = f32[2]{0:T(128)S(1)} all-reduce(f32[2]{0:T(128)S(1)} %psum.29), channel_id=1, replica_groups=mesh['tok_0'=4,'tok_1'=8,'tok_2'=4,'exp'=2] {'tok_2'}, use_global_device_ids=true, to_apply=%region_5.6 | all-reduce | flops 2 | bytes 16 | tf_op jit(solution)/shard_map/psum | solution.py:43
  312.1 5.9 %psum.31 = f32[2]{0:T(128)S(1)} all-reduce(f32[2]{0:T(128)S(1)} %psum.30), channel_id=1, replica_groups=mesh['tok_0'=4,'tok_1'=8,'tok_2'=4,'exp'=2] {'exp'}, use_global_device_ids=true, to_apply=%region_6.7 | all-reduce | flops 2 | bytes 16 | tf_op jit(solution)/shard_map/psum | solution.py:43
  318.0 0.6 dynamic_slice.11
  319.2 0.0 all-to-all-done.2
  319.2 6.0 %broadcast_multiply_fusion = f32[4,112,3584]{2,1,0:T(8,128)} fusion(f32[4,112,3584]{2,1,0:T(8,128)} %all-to-all-done.2, f32[]{:T(128)} %bitcast.12), kind=kLoop, calls=%fused_computation.2 | loop fusion | flops 1605632 | bytes 12845060 | tf_op jit(solution)/shard_map/mul | solution.py:69
  325.2 7.9 %reshape.86 = f32[4,112,28,128]{3,2,1,0:T(8,128)} reshape(f32[4,112,3584]{2,1,0:T(8,128)} %broadcast_multiply_fusion) | data formatting | bytes 12845056 | tf_op jit(solution)/shard_map/reshape | solution.py:70
  333.1 12.1 %copy.20 = f32[112,28,4,128]{3,2,1,0:T(4,128)} copy(f32[112,28,4,128]{3,1,0,2:T(8,128)} %bitcast.28) | data formatting | bytes 12845056 | tf_op jit(solution)/shard_map/transpose | solution.py:70
  345.2 8.2 %reshape.87 = f32[1,112,14336]{2,1,0:T(8,128)} reshape(f32[112,28,4,128]{3,2,1,0:T(4,128)} %copy.20) | data formatting | bytes 12845056 | tf_op jit(solution)/shard_map/reshape | solution.py:71
  (7 shorter events, 0.1 us)
Async XLA Ops:
  6.5 1.0 copy-start
  24.1 173.7 %all-to-all-start.1 = ((bf16[32,32,3584]{2,1,0:T(8,128)(2,1)}), bf16[32,32,3584]{2,1,0:T(8,128)(2,1)}, u32[]{:S(2)}, u32[]{:S(2)}) async-start(bf16[32,32,3584]{2,1,0:T(8,128)(2,1)} %stack.3), calls=%async_computation.1 | async-start | bytes 14680064 | tf_op jit(solution)/shard_map/all_to_all | solution.py:46
  35.3 188.1 %all-gather.3.cloned.1.call-start = ((), (), s32[]{:S(2)}) async-start(), calls=%async_computation.3 | async-start | bytes 1310720 | tf_op jit(solution)/shard_map/all_gather | solution.py:55
  234.6 84.6 %all-to-all-start.2 = ((f32[4,112,3584]{2,1,0:T(8,128)}), f32[4,112,3584]{2,1,0:T(8,128)}, u32[]{:S(2)}, u32[]{:S(2)}) async-start(f32[4,112,3584]{2,1,0:T(8,128)} %fusion.8), calls=%async_computation.2 | async-start | bytes 12845056 | tf_op jit(solution)/shard_map/all_to_all | solution.py:62
Sparse Core Ops, SparseCore 0:
  199.7 23.6 all-gather.2
